TPU v7x, 32 devices: a whole 2x2x4 slice. The times are simulated.
32 devices in a mesh: head: 4 (over x, core), inner: 2 (over y), outer: 4 (over z).
Axes of the slice: x: 2, y: 2, z: 4, core: 2. Of those that a mesh axis runs over, the one named last changes fastest.
Arguments:
- rotated_asking_matrix: bfloat16 [4096, 32, 128], P(('head', 'inner', 'outer')), may hold values from -12 to 12
- rotated_lookup_matrix: bfloat16 [4096, 8, 128], P(('head', 'inner', 'outer')), may hold values from -6 to 6
- content_matrix: bfloat16 [4096, 8, 128], P(('head', 'inner', 'outer')), may hold values from -6 to 6
Outputs:
- attended: bfloat16 [4096, 32, 128], P(('head', 'inner', 'outer'))
All inputs are finite; a program needn't handle non-finite values.
Results may differ from a plain program's by a relative error of at most 0.001.
Values may be sent and summed in bfloat16 or wider, within the bound.
A program may use at most 64 MiB of HBM per device.

v0:
```python
import math

import jax
import jax.numpy as jnp
from jax import lax
from jax.sharding import PartitionSpec as P


def for_sending(x):
    def short(part):
        return part.astype(jnp.bfloat16) if part.dtype == jnp.float32 else part

    return jax.tree.map(short, x)


def passed_along(x, axis, by):
    size = lax.axis_size(axis)
    return lax.ppermute(x, axis, [(i, (i + by) % size) for i in range(size)])


def shards(rotated_asking_matrix, rotated_lookup_matrix, content_matrix):
    query_local, key_local, value_local = (
        lax.all_to_all(rotated_asking_matrix, "head", split_axis=1, concat_axis=0, tiled=True),
        lax.all_to_all(rotated_lookup_matrix, "head", split_axis=1, concat_axis=0, tiled=True),
        lax.all_to_all(content_matrix, "head", split_axis=1, concat_axis=0, tiled=True),
    )
    inner_count = lax.axis_size("inner")
    outer_count = lax.axis_size("outer")
    cycle_count = inner_count * outer_count
    block_len = rotated_asking_matrix.shape[0]
    local_len = key_local.shape[0]
    kv_heads = key_local.shape[1]
    group_size = query_local.shape[1] // kv_heads
    head_dim = query_local.shape[2]
    grouped = query_local.reshape(local_len, kv_heads, group_size, head_dim)
    inner_self = lax.axis_index("inner")
    outer_self = lax.axis_index("outer")
    offsets = jnp.arange(local_len, dtype=jnp.int32)
    score_scale = 1.0 / math.sqrt(head_dim)

    def places(cycle_id):
        return (offsets // block_len * cycle_count + cycle_id) * block_len + offsets % block_len

    query_pos = places(inner_self * outer_count + outer_self)

    def absorb(carry, key_block, value_block, key_pos):
        run_max, run_sum, accum = carry
        scores = (
            jnp.einsum("tkgd,skd->kgts", grouped, key_block, preferred_element_type=jnp.float32)
            * score_scale
        )
        allowed = key_pos[None, :] <= query_pos[:, None]
        scores = jnp.where(allowed, scores, -1e30)
        new_max = jnp.maximum(run_max, jnp.max(scores, axis=-1))
        factor = jnp.exp(run_max - new_max)
        weights = jnp.where(allowed, jnp.exp(scores - new_max[..., None]), 0.0)
        run_sum = run_sum * factor + jnp.sum(weights, axis=-1)
        mixed = jnp.einsum(
            "kgts,skd->kgtd",
            weights,
            value_block.astype(jnp.float32),
            precision=lax.Precision.HIGHEST,
        )
        accum = accum * factor[..., None] + mixed
        return (new_max, run_sum, accum)

    def sweep(carry, window, outer_step):
        outer_source = (outer_self - outer_step) % outer_count

        def cycle_pos(inner_source):
            return places(inner_source * outer_count + outer_source)

        carry = absorb(carry, window[0], window[1], cycle_pos(inner_self))

        def inner_body(inner_step, loop_state):
            carry_state, moving = loop_state
            moving = jax.tree.map(
                lambda part, own: part.astype(own.dtype),
                passed_along(for_sending(moving), "inner", 1),
                moving,
            )
            key_pos = cycle_pos((inner_self - inner_step) % inner_count)
            carry_state = absorb(carry_state, moving[0], moving[1], key_pos)
            return (carry_state, moving)

        carry, moving = lax.fori_loop(1, inner_count, inner_body, (carry, window))
        return carry

    carry = (
        jnp.full((kv_heads, group_size, local_len), -1e30, jnp.float32),
        jnp.zeros((kv_heads, group_size, local_len), jnp.float32),
        jnp.zeros((kv_heads, group_size, local_len, head_dim), jnp.float32),
    )
    window = jnp.stack([key_local, value_local])

    def outer_body(outer_step, loop_state):
        carry_state, current = loop_state
        upcoming = jax.tree.map(
            lambda part, own: part.astype(own.dtype),
            passed_along(for_sending(current), "outer", 1),
            current,
        )
        carry_state = sweep(carry_state, current, outer_step)
        return (carry_state, upcoming)

    carry, window = lax.fori_loop(0, outer_count - 1, outer_body, (carry, window))
    carry = sweep(carry, window, outer_count - 1)
    run_max, run_sum, accum = carry
    result = (accum / run_sum[..., None]).astype(jnp.bfloat16)
    result = result.transpose(2, 0, 1, 3).reshape(local_len, kv_heads * group_size, head_dim)
    return lax.all_to_all(result, "head", split_axis=0, concat_axis=1, tiled=True)


def solution(mesh):
    placed = (
        P(("head", "inner", "outer"), None, None),
        P(("head", "inner", "outer"), None, None),
        P(("head", "inner", "outer"), None, None),
    )
    return jax.shard_map(
        shards,
        mesh=mesh,
        in_specs=placed,
        out_specs=P(("head", "inner", "outer"), None, None),
        check_vma=False,
    )
```

profile of v0, /device:TPU:7, one launch (start us, length us, event | category | flops | bytes accessed | tf_op | source)
XLA Modules:
  0.0 201.3 jit_solution(4616779751320213047)
XLA Ops:
  0.0 1.7 copy.14
  1.7 4.2 %all-to-all-start = ((bf16[128,8,128]{2,0,1:T(8,128)(2,1)}), bf16[128,8,128]{2,0,1:T(8,128)(2,1)S(1)}, u32[]{:S(2)}, u32[]{:S(2)}) async-start(bf16[128,8,128]{2,0,1:T(8,128)(2,1)} %copy.14), calls=%async_computation | async-start | bytes 524288 | tf_op jit(solution)/shard_map/all_to_all | solution.py:24
  5.9 1.7 copy.16
  7.6 2.5 %all-to-all-done = bf16[128,8,128]{2,0,1:T(8,128)(2,1)S(1)} async-done(((bf16[128,8,128]{2,0,1:T(8,128)(2,1)}), bf16[128,8,128]{2,0,1:T(8,128)(2,1)S(1)}, u32[]{:S(2)}, u32[]{:S(2)}) %all-to-all-start) | async-done | bytes 262176 | tf_op jit(solution)/shard_map/all_to_all | solution.py:24
  10.0 5.2 %all-to-all-start.1 = ((bf16[128,8,128]{2,0,1:T(8,128)(2,1)}), bf16[128,8,128]{2,0,1:T(8,128)(2,1)S(1)}, u32[]{:S(2)}, u32[]{:S(2)}) async-start(bf16[128,8,128]{2,0,1:T(8,128)(2,1)} %copy.16), calls=%async_computation.1 | async-start | bytes 524288 | tf_op jit(solution)/shard_map/all_to_all | solution.py:25
  15.3 2.6 %copy.18 = bf16[128,32,128]{2,0,1:T(8,128)(2,1)} copy(bf16[128,32,128]{2,1,0:T(8,128)(2,1)} %param.5) | data formatting | bytes 2097152 | tf_op args[0]
  17.9 1.6 all-to-all-done.1
  19.4 5.3 %all-to-all-start.2 = ((bf16[128,32,128]{2,0,1:T(8,128)(2,1)}), bf16[128,32,128]{2,0,1:T(8,128)(2,1)S(1)}, u32[]{:S(2)}, u32[]{:S(2)}) async-start(bf16[128,32,128]{2,0,1:T(8,128)(2,1)} %copy.18), calls=%async_computation.2 | async-start | bytes 2097152 | tf_op jit(solution)/shard_map/all_to_all | solution.py:23
  24.9 0.1 pad_maximum_fusion
  24.9 12.4 %all-to-all-done.2 = bf16[128,32,128]{2,0,1:T(8,128)(2,1)S(1)} async-done(((bf16[128,32,128]{2,0,1:T(8,128)(2,1)}), bf16[128,32,128]{2,0,1:T(8,128)(2,1)S(1)}, u32[]{:S(2)}, u32[]{:S(2)}) %all-to-all-start.2) | async-done | bytes 1048608 | tf_op jit(solution)/shard_map/all_to_all | solution.py:23
  37.4 0.1 copy.19
  37.5 109.2 %while.49 = (s32[]{:T(128)}, f32[2,4,512]{2,1,0:T(4,128)S(1)}, f32[2,4,512]{2,1,0:T(4,128)S(1)}, f32[2,4,512,128]{3,2,1,0:T(8,128)}, bf16[2,512,2,128]{3,1,2,0:T...) while((s32[]{:T(128)}, f32[2,4,512]{2,1,0:T(4,128)S(1)}, ...), condition=%wide.region_5.6_spmd.clone.clone, body=%wide.region_0.5_spmd.clone.clone.sunk | while | flops 7569716736 | bytes 86422968 | solution.py:106
  37.5 0.1 collective-permute-start
  37.6 1.5 collective-permute-start.1
  39.2 0.4 broadcast_compare_fusion.5
  39.5 1.5 fusion.113
  41.1 9.4 %collective-permute-done = bf16[2,512,2,128]{3,1,2,0:T(8,128)(2,1)S(1)} collective-permute-done((bf16[2,512,2,128]{3,1,2,0:T(8,128)(2,1)S(1)}, bf16[2,512,2,128]{3,1,2,0:T(8,128)(2,1)S(1)}, u32[]{:S(2)}, u32[]{:S(2)}) %collective-permute-start) | collective-permute-done | bytes 524320 | tf_op jit(solution)/shard_map/while/body/eval_jaxpr/while/body/eval_jaxpr/ppermute | solution.py:18
  50.5 1.5 fusion.112
  52.0 7.6 %fusion.117 = f32[2,4,512,128]{3,2,1,0:T(8,128)S(1)} fusion(f32[2,512,512,4]{2,1,3,0:T(8,128)S(1)} %get-tuple-element.740, f32[2,4,512]{2,1,0:T(4,128)S(1)} %get-tuple-element.741, pred[512,512]{0,1:T(8,128)(4,1)S(1)} %get-tuple-element.737, bf16[2,512,2,128]{3,1,2,0:T(8,128)(2,1)S(1)} %copy.47), kind=kOutput, calls=%fused_computation.11.clone.1 | convolution fusion | flops 3229614080 | bytes 11026432 | tf_op jit(solution)/shard_map/while/body/eval_jaxpr/kgts,skd->kgtd/dot_general | solution.py:58
  59.7 0.0 copy-start
  59.7 4.1 %fusion.115 = (f32[2,4,512]{2,1,0:T(4,128)S(1)}, f32[2,4,512]{2,1,0:T(4,128)S(1)}) fusion(f32[2,512,512,4]{2,1,3,0:T(8,128)S(1)} %get-tuple-element.740, f32[2,4,512]{2,1,0:T(4,128)S(1)} %get-tuple-element.741, pred[512,512]{0,1:T(8,128)(4,1)S(1)} %get-tuple-element.737, f32[2,4,512]{2,1,0:T(4,128)S(1)} %get-tuple-element.777, ...), kind=kLoop, calls=%fused_computation.12.clone.1 | loop fusion | flops 20963328 | bytes 17367040 | tf_op jit(solution)/shard_map/while/body/eval_jaxpr/reduce_sum | solution.py:57
  63.8 0.0 copy-done
  63.8 9.6 %fusion.118 = f32[2,4,512,128]{3,2,1,0:T(8,128)S(1)} fusion(f32[2,4,512,128]{3,2,1,0:T(8,128)S(1)} %fusion.117, f32[2,4,512,128]{3,2,1,0:T(8,128)S(1)} %copy-done, f32[2,512,512,4]{2,1,3,0:T(8,128)S(1)} %get-tuple-element.742, f32[2,4,512]{2,1,0:T(4,128)S(1)} %get-tuple-element.777, pred[512,512]{0,1:T(8,128)(4,1)S(1)} %get-tuple-element.735, ...), kind=kOutput, calls=%fused_computation.28.clone.1 | convolution fusion | flops 3232235520 | bytes 15253505 | tf_op jit(solution)/shard_map/while/body/eval_jaxpr/while/body/eval_jaxpr/kgts,skd->kgtd/dot_general | solution.py:58
  73.4 0.0 copy-start.1
  73.4 0.0 collective-permute-done.1
  73.4 1.3 copy-done.1
  74.8 0.4 collective-permute-start
  75.1 1.2 collective-permute-start.1
  76.4 0.4 broadcast_compare_fusion.5
  76.8 1.5 fusion.113
  78.3 8.5 %collective-permute-done = bf16[2,512,2,128]{3,1,2,0:T(8,128)(2,1)S(1)} collective-permute-done((bf16[2,512,2,128]{3,1,2,0:T(8,128)(2,1)S(1)}, bf16[2,512,2,128]{3,1,2,0:T(8,128)(2,1)S(1)}, u32[]{:S(2)}, u32[]{:S(2)}) %collective-permute-start) | collective-permute-done | bytes 524320 | tf_op jit(solution)/shard_map/while/body/eval_jaxpr/while/body/eval_jaxpr/ppermute | solution.py:18
  86.8 1.5 fusion.112
  88.4 7.6 %fusion.117 = f32[2,4,512,128]{3,2,1,0:T(8,128)S(1)} fusion(f32[2,512,512,4]{2,1,3,0:T(8,128)S(1)} %get-tuple-element.740, f32[2,4,512]{2,1,0:T(4,128)S(1)} %get-tuple-element.741, pred[512,512]{0,1:T(8,128)(4,1)S(1)} %get-tuple-element.737, bf16[2,512,2,128]{3,1,2,0:T(8,128)(2,1)S(1)} %copy.47), kind=kOutput, calls=%fused_computation.11.clone.1 | convolution fusion | flops 3229614080 | bytes 11026432 | tf_op jit(solution)/shard_map/while/body/eval_jaxpr/kgts,skd->kgtd/dot_general | solution.py:58
  96.0 0.0 copy-start
  96.0 4.1 %fusion.115 = (f32[2,4,512]{2,1,0:T(4,128)S(1)}, f32[2,4,512]{2,1,0:T(4,128)S(1)}) fusion(f32[2,512,512,4]{2,1,3,0:T(8,128)S(1)} %get-tuple-element.740, f32[2,4,512]{2,1,0:T(4,128)S(1)} %get-tuple-element.741, pred[512,512]{0,1:T(8,128)(4,1)S(1)} %get-tuple-element.737, f32[2,4,512]{2,1,0:T(4,128)S(1)} %get-tuple-element.777, ...), kind=kLoop, calls=%fused_computation.12.clone.1 | loop fusion | flops 20963328 | bytes 17367040 | tf_op jit(solution)/shard_map/while/body/eval_jaxpr/reduce_sum | solution.py:57
  100.2 0.0 copy-done
  100.2 9.6 %fusion.118 = f32[2,4,512,128]{3,2,1,0:T(8,128)S(1)} fusion(f32[2,4,512,128]{3,2,1,0:T(8,128)S(1)} %fusion.117, f32[2,4,512,128]{3,2,1,0:T(8,128)S(1)} %copy-done, f32[2,512,512,4]{2,1,3,0:T(8,128)S(1)} %get-tuple-element.742, f32[2,4,512]{2,1,0:T(4,128)S(1)} %get-tuple-element.777, pred[512,512]{0,1:T(8,128)(4,1)S(1)} %get-tuple-element.735, ...), kind=kOutput, calls=%fused_computation.28.clone.1 | convolution fusion | flops 3232235520 | bytes 15253505 | tf_op jit(solution)/shard_map/while/body/eval_jaxpr/while/body/eval_jaxpr/kgts,skd->kgtd/dot_general | solution.py:58
  109.7 0.0 copy-start.1
  109.8 0.0 collective-permute-done.1
  109.8 1.3 copy-done.1
  111.1 0.6 collective-permute-start
  111.8 1.0 collective-permute-start.1
  112.8 0.4 broadcast_compare_fusion.5
  113.2 1.5 fusion.113
  114.7 7.6 %collective-permute-done = bf16[2,512,2,128]{3,1,2,0:T(8,128)(2,1)S(1)} collective-permute-done((bf16[2,512,2,128]{3,1,2,0:T(8,128)(2,1)S(1)}, bf16[2,512,2,128]{3,1,2,0:T(8,128)(2,1)S(1)}, u32[]{:S(2)}, u32[]{:S(2)}) %collective-permute-start) | collective-permute-done | bytes 524320 | tf_op jit(solution)/shard_map/while/body/eval_jaxpr/while/body/eval_jaxpr/ppermute | solution.py:18
  122.4 1.5 fusion.112
  123.9 7.6 %fusion.117 = f32[2,4,512,128]{3,2,1,0:T(8,128)S(1)} fusion(f32[2,512,512,4]{2,1,3,0:T(8,128)S(1)} %get-tuple-element.740, f32[2,4,512]{2,1,0:T(4,128)S(1)} %get-tuple-element.741, pred[512,512]{0,1:T(8,128)(4,1)S(1)} %get-tuple-element.737, bf16[2,512,2,128]{3,1,2,0:T(8,128)(2,1)S(1)} %copy.47), kind=kOutput, calls=%fused_computation.11.clone.1 | convolution fusion | flops 3229614080 | bytes 11026432 | tf_op jit(solution)/shard_map/while/body/eval_jaxpr/kgts,skd->kgtd/dot_general | solution.py:58
  131.6 0.0 copy-start
  131.6 4.1 %fusion.115 = (f32[2,4,512]{2,1,0:T(4,128)S(1)}, f32[2,4,512]{2,1,0:T(4,128)S(1)}) fusion(f32[2,512,512,4]{2,1,3,0:T(8,128)S(1)} %get-tuple-element.740, f32[2,4,512]{2,1,0:T(4,128)S(1)} %get-tuple-element.741, pred[512,512]{0,1:T(8,128)(4,1)S(1)} %get-tuple-element.737, f32[2,4,512]{2,1,0:T(4,128)S(1)} %get-tuple-element.777, ...), kind=kLoop, calls=%fused_computation.12.clone.1 | loop fusion | flops 20963328 | bytes 17367040 | tf_op jit(solution)/shard_map/while/body/eval_jaxpr/reduce_sum | solution.py:57
  135.7 9.6 %fusion.118 = f32[2,4,512,128]{3,2,1,0:T(8,128)S(1)} fusion(f32[2,4,512,128]{3,2,1,0:T(8,128)S(1)} %fusion.117, f32[2,4,512,128]{3,2,1,0:T(8,128)S(1)} %copy-done, f32[2,512,512,4]{2,1,3,0:T(8,128)S(1)} %get-tuple-element.742, f32[2,4,512]{2,1,0:T(4,128)S(1)} %get-tuple-element.777, pred[512,512]{0,1:T(8,128)(4,1)S(1)} %get-tuple-element.735, ...), kind=kOutput, calls=%fused_computation.28.clone.1 | convolution fusion | flops 3232235520 | bytes 15253505 | tf_op jit(solution)/shard_map/while/body/eval_jaxpr/while/body/eval_jaxpr/kgts,skd->kgtd/dot_general | solution.py:58
  145.3 0.0 collective-permute-done.1
  145.3 1.3 copy-done.1
  146.6 0.8 collective-permute-start.2
  147.5 0.4 broadcast_compare_fusion.3
  147.8 1.5 fusion.55
  149.4 7.6 %collective-permute-done.2 = bf16[2,512,2,128]{3,1,2,0:T(8,128)(2,1)S(1)} collective-permute-done((bf16[2,512,2,128]{3,1,2,0:T(8,128)(2,1)S(1)}, bf16[2,512,2,128]{3,1,2,0:T(8,128)(2,1)S(1)}, u32[]{:S(2)}, u32[]{:S(2)}) %collective-permute-start.2) | collective-permute-done | bytes 524320 | tf_op jit(solution)/shard_map/while/body/eval_jaxpr/ppermute | solution.py:18
  156.9 1.5 fusion.56
  158.5 7.6 %fusion.58 = f32[2,4,512,128]{3,2,1,0:T(8,128)S(1)} fusion(f32[2,512,512,4]{2,1,3,0:T(8,128)S(1)} %get-tuple-element.649, f32[2,4,512]{2,1,0:T(4,128)S(1)} %bitcast.171, pred[512,512]{0,1:T(8,128)(4,1)S(1)} %get-tuple-element.644, bf16[2,512,2,128]{3,1,2,0:T(8,128)(2,1)S(1)} %get-tuple-element.515), kind=kOutput, calls=%fused_computation.78 | convolution fusion | flops 3229614080 | bytes 11026432 | tf_op jit(solution)/shard_map/kgts,skd->kgtd/dot_general | solution.py:58
  166.1 4.3 %fusion.57 = (f32[2,4,512]{2,1,0:T(4,128)S(1)}, f32[2,4,512]{2,1,0:T(4,128)S(1)}) fusion(f32[2,512,512,4]{2,1,3,0:T(8,128)S(1)} %get-tuple-element.649, f32[2,4,512]{2,1,0:T(4,128)S(1)} %bitcast.172, pred[512,512]{0,1:T(8,128)(4,1)S(1)} %get-tuple-element.644, f32[2,4,512]{2,1,0:T(4,128)S(1)} %bitcast.169, f32[2,512,512,4]{2,1,3,0:T(8,128)S(1)} %get-tuple-element.647, ...), kind=kLoop, calls=%fused_computation.77 | loop fusion | flops 20963328 | bytes 17367040 | tf_op jit(solution)/shard_map/reduce_sum | solution.py:57
  170.4 0.0 copy-done.2
  170.4 9.4 %divide_convert_fusion = bf16[2,4,512,128]{3,2,1,0:T(8,128)(2,1)S(1)} fusion(f32[2,4,512,128]{3,2,1,0:T(8,128)S(1)} %fusion.58, f32[2,4,512,128]{3,2,1,0:T(8,128)S(1)} %copy-done.2, f32[2,512,512,4]{2,1,3,0:T(8,128)S(1)} %get-tuple-element.647, f32[2,4,512]{2,1,0:T(4,128)S(1)} %bitcast.170, pred[512,512]{0,1:T(8,128)(4,1)S(1)} %get-tuple-element.645, ...), kind=kOutput, calls=%fused_computation.91 | convolution fusion | flops 3232759808 | bytes 14221312 | tf_op jit(solution)/shard_map/while/body/eval_jaxpr/kgts,skd->kgtd/dot_general | solution.py:58
  179.8 0.7 copy.22
  180.5 19.3 %all_to_all.63 = bf16[512,8,128]{2,1,0:T(8,128)(2,1)S(1)} all-to-all(bf16[512,8,128]{2,1,0:T(8,128)(2,1)S(1)} %copy.22), channel_id=1, replica_groups=mesh['head'=4,'inner'=2,'outer'=4] {'head'}, dimensions={0} | all-to-all | bytes 2097152 | tf_op jit(solution)/shard_map/all_to_all | solution.py:111
  199.8 1.1 copy.37
  (34 shorter events, 0.5 us)
Async XLA Ops:
  1.7 8.4 %all-to-all-start = ((bf16[128,8,128]{2,0,1:T(8,128)(2,1)}), bf16[128,8,128]{2,0,1:T(8,128)(2,1)S(1)}, u32[]{:S(2)}, u32[]{:S(2)}) async-start(bf16[128,8,128]{2,0,1:T(8,128)(2,1)} %copy.14), calls=%async_computation | async-start | bytes 524288 | tf_op jit(solution)/shard_map/all_to_all | solution.py:24
  10.0 9.4 %all-to-all-start.1 = ((bf16[128,8,128]{2,0,1:T(8,128)(2,1)}), bf16[128,8,128]{2,0,1:T(8,128)(2,1)S(1)}, u32[]{:S(2)}, u32[]{:S(2)}) async-start(bf16[128,8,128]{2,0,1:T(8,128)(2,1)} %copy.16), calls=%async_computation.1 | async-start | bytes 524288 | tf_op jit(solution)/shard_map/all_to_all | solution.py:25
  19.4 17.9 %all-to-all-start.2 = ((bf16[128,32,128]{2,0,1:T(8,128)(2,1)}), bf16[128,32,128]{2,0,1:T(8,128)(2,1)S(1)}, u32[]{:S(2)}, u32[]{:S(2)}) async-start(bf16[128,32,128]{2,0,1:T(8,128)(2,1)} %copy.18), calls=%async_computation.2 | async-start | bytes 2097152 | tf_op jit(solution)/shard_map/all_to_all | solution.py:23
  37.5 12.9 %collective-permute-start = (bf16[2,512,2,128]{3,1,2,0:T(8,128)(2,1)S(1)}, bf16[2,512,2,128]{3,1,2,0:T(8,128)(2,1)S(1)}, u32[]{:S(2)}, u32[]{:S(2)}) collective-permute-start(bf16[2,512,2,128]{3,1,2,0:T(8,128)(2,1)S(1)} %copy.47), channel_id=1, source_target_pairs={{0,4},{4,0},{1,5},{5,1},{2,6},{6,2},{3,7},{7,3},{8,12},{12,8},{9,1... | collective-permute-start | bytes 1572872 | tf_op jit(solution)/shard_map/while/body/eval_jaxpr/while/body/eval_jaxpr/ppermute | solution.py:18
  37.6 35.8 %collective-permute-start.1 = (bf16[2,512,2,128]{3,1,2,0:T(8,128)(2,1)S(1)}, bf16[2,512,2,128]{3,1,2,0:T(8,128)(2,1)S(1)}, u32[]{:S(2)}, u32[]{:S(2)}) collective-permute-start(bf16[2,512,2,128]{3,1,2,0:T(8,128)(2,1)S(1)} %copy.47), channel_id=1, source_target_pairs={{0,1},{1,2},{2,3},{3,0},{4,5},{5,6},{6,7},{7,4},{8,9},{9,10},{10,1... | collective-permute-start | bytes 1572872 | tf_op jit(solution)/shard_map/while/body/eval_jaxpr/ppermute | solution.py:18
  59.7 4.1 %copy-start = (f32[2,4,512,128]{3,2,1,0:T(8,128)S(1)}, f32[2,4,512,128]{3,2,1,0:T(8,128)}, u32[]{:S(2)}) copy-start(f32[2,4,512,128]{3,2,1,0:T(8,128)} %get-tuple-element.765) | copy-start | bytes 6291460 | tf_op jit(solution)/shard_map/while
  73.4 1.4 copy-start.1
  74.8 12.1 %collective-permute-start = (bf16[2,512,2,128]{3,1,2,0:T(8,128)(2,1)S(1)}, bf16[2,512,2,128]{3,1,2,0:T(8,128)(2,1)S(1)}, u32[]{:S(2)}, u32[]{:S(2)}) collective-permute-start(bf16[2,512,2,128]{3,1,2,0:T(8,128)(2,1)S(1)} %copy.47), channel_id=1, source_target_pairs={{0,4},{4,0},{1,5},{5,1},{2,6},{6,2},{3,7},{7,3},{8,12},{12,8},{9,1... | collective-permute-start | bytes 1572872 | tf_op jit(solution)/shard_map/while/body/eval_jaxpr/while/body/eval_jaxpr/ppermute | solution.py:18
  75.1 34.6 %collective-permute-start.1 = (bf16[2,512,2,128]{3,1,2,0:T(8,128)(2,1)S(1)}, bf16[2,512,2,128]{3,1,2,0:T(8,128)(2,1)S(1)}, u32[]{:S(2)}, u32[]{:S(2)}) collective-permute-start(bf16[2,512,2,128]{3,1,2,0:T(8,128)(2,1)S(1)} %copy.47), channel_id=1, source_target_pairs={{0,1},{1,2},{2,3},{3,0},{4,5},{5,6},{6,7},{7,4},{8,9},{9,10},{10,1... | collective-permute-start | bytes 1572872 | tf_op jit(solution)/shard_map/while/body/eval_jaxpr/ppermute | solution.py:18
  96.0 4.1 %copy-start = (f32[2,4,512,128]{3,2,1,0:T(8,128)S(1)}, f32[2,4,512,128]{3,2,1,0:T(8,128)}, u32[]{:S(2)}) copy-start(f32[2,4,512,128]{3,2,1,0:T(8,128)} %get-tuple-element.765) | copy-start | bytes 6291460 | tf_op jit(solution)/shard_map/while
  109.7 1.4 copy-start.1
  111.1 11.2 %collective-permute-start = (bf16[2,512,2,128]{3,1,2,0:T(8,128)(2,1)S(1)}, bf16[2,512,2,128]{3,1,2,0:T(8,128)(2,1)S(1)}, u32[]{:S(2)}, u32[]{:S(2)}) collective-permute-start(bf16[2,512,2,128]{3,1,2,0:T(8,128)(2,1)S(1)} %copy.47), channel_id=1, source_target_pairs={{0,4},{4,0},{1,5},{5,1},{2,6},{6,2},{3,7},{7,3},{8,12},{12,8},{9,1... | collective-permute-start | bytes 1572872 | tf_op jit(solution)/shard_map/while/body/eval_jaxpr/while/body/eval_jaxpr/ppermute | solution.py:18
  111.8 33.5 %collective-permute-start.1 = (bf16[2,512,2,128]{3,1,2,0:T(8,128)(2,1)S(1)}, bf16[2,512,2,128]{3,1,2,0:T(8,128)(2,1)S(1)}, u32[]{:S(2)}, u32[]{:S(2)}) collective-permute-start(bf16[2,512,2,128]{3,1,2,0:T(8,128)(2,1)S(1)} %copy.47), channel_id=1, source_target_pairs={{0,1},{1,2},{2,3},{3,0},{4,5},{5,6},{6,7},{7,4},{8,9},{9,10},{10,1... | collective-permute-start | bytes 1572872 | tf_op jit(solution)/shard_map/while/body/eval_jaxpr/ppermute | solution.py:18
  131.6 4.1 %copy-start = (f32[2,4,512,128]{3,2,1,0:T(8,128)S(1)}, f32[2,4,512,128]{3,2,1,0:T(8,128)}, u32[]{:S(2)}) copy-start(f32[2,4,512,128]{3,2,1,0:T(8,128)} %get-tuple-element.765) | copy-start | bytes 6291460 | tf_op jit(solution)/shard_map/while
  145.3 1.4 copy-start.1
  146.6 10.3 %collective-permute-start.2 = (bf16[2,512,2,128]{3,1,2,0:T(8,128)(2,1)S(1)}, bf16[2,512,2,128]{3,1,2,0:T(8,128)(2,1)S(1)}, u32[]{:S(2)}, u32[]{:S(2)}) collective-permute-start(bf16[2,512,2,128]{3,1,2,0:T(8,128)(2,1)S(1)} %get-tuple-element.515), channel_id=1, source_target_pairs={{0,4},{4,0},{1,5},{5,1},{2,6},{6,2},{3,7},{7,3},{8,12},{12,8},{9,1... | collective-permute-start | bytes 1572872 | tf_op jit(solution)/shard_map/while/body/eval_jaxpr/ppermute | solution.py:18
  166.1 4.3 %copy-start.2 = (f32[2,4,512,128]{3,2,1,0:T(8,128)S(1)}, f32[2,4,512,128]{3,2,1,0:T(8,128)}, u32[]{:S(2)}) copy-start(f32[2,4,512,128]{3,2,1,0:T(8,128)} %get-tuple-element.513) | copy-start | bytes 6291460
where the time goes:
time: 205 us; the launch traced here: 201 us
  matrix products  80.9 us (39%)
  waiting for transfers between devices  49.6 us (24%)
  starting transfers between devices  20.4 us (10%)
  blocking collectives  19.3 us (9%)
  other arithmetic  18.3 us (9%)
  local copies, waits for them, and re-layouts  12.1 us (6%)
    dot_general x8, matrix products, absorb(): jnp.einsum('kgts,skd->kgtd', weights, value_block.astype(jnp.float32), pr...  68.5 us
    ppermute x7, waiting for transfers between devices, passed_along(): return lax.ppermute(x, axis, [(i, (i + by) % size) for i in range(size)])  33.1 us
    all_to_all x1, blocking collectives, shards(): lax.all_to_all(result, 'head', split_axis=0, concat_axis=1, tiled=True)  19.3 us
    reduce_sum x4, other arithmetic, absorb(): run_sum = run_sum * factor + jnp.sum(weights, axis=-1)  16.4 us
    all_to_all x1, waiting for transfers between devices, shards(): lax.all_to_all(rotated_asking_matrix, 'head', split_axis=1, concat_axis=0...  12.4 us
    dot_general x8, matrix products, absorb(): jnp.einsum('tkgd,skd->kgts', grouped, key_block, preferred_element_type=j...  12.3 us
    unnamed x5, local copies, waits for them, and re-layouts  5.97 us
    ppermute x7, starting transfers between devices, passed_along(): return lax.ppermute(x, axis, [(i, (i + by) % size) for i in range(size)])  5.6 us
  transfers between devices with their start and end apart: 10, of which 7 were waited for; matrix products, arithmetic and copies ran while one was open for 40% of the time, Pallas kernels for 0%

commit v1 on v0

v1 whole, which is shorter than its diff:
```python
import functools
import math

import jax
import jax.numpy as jnp
from jax import lax
from jax.experimental import pallas as pl
from jax.experimental.pallas import tpu as pltpu
from jax.sharding import PartitionSpec as P

MESH = pl.DeviceIdType.MESH


def kernel(sizes, q_ref, kv_ref, out_ref, q_buf, kv_buf, o_buf, m_ref, acc_ref,
           q_send, q_recv, kv_send, kv_recv, up_send, down_send, o_send, o_recv):
    head_n, inner_n, outer_n, split, members, planes, block, group, dim = sizes
    rest = inner_n // split
    wide = group * dim
    pair = 2 * dim
    rows = group * block
    keys = planes * block
    head = lax.axis_index("head")
    inner = lax.axis_index("inner")
    outer = lax.axis_index("outer")
    me = head * split + inner // rest
    plane = (inner % rest) * outer_n + outer

    def member_id(m):
        return (m // split, (m % split) * rest + inner % rest, outer)

    def plane_id(p):
        return (head, (inner // rest) * rest + p // outer_n, p % outer_n)

    def lanes(index, width):
        return pl.ds(pl.multiple_of(index * width, dim), width)

    def slot(r, p):
        return kv_buf.at[pl.ds(pl.multiple_of((r * planes + p) * block, block), block), :]

    def kv_copy(j):
        to = (me + j) % members
        return pltpu.make_async_remote_copy(
            src_ref=kv_ref.at[:, lanes(to, pair)], dst_ref=slot(me, plane),
            send_sem=kv_send.at[j], recv_sem=kv_recv.at[me, plane],
            device_id=member_id(to), device_id_type=MESH)

    def q_copy(j):
        to = (me + j) % members
        return pltpu.make_async_remote_copy(
            src_ref=q_ref.at[:, lanes(to, wide)], dst_ref=q_buf.at[me],
            send_sem=q_send.at[j], recv_sem=q_recv.at[me],
            device_id=member_id(to), device_id_type=MESH)

    def pass_up(r, p):
        return pltpu.make_async_remote_copy(
            src_ref=slot(r, p), dst_ref=slot(r, p),
            send_sem=up_send.at[r, p], recv_sem=kv_recv.at[r, p],
            device_id=plane_id(plane + 1), device_id_type=MESH)

    def pass_down(r, p):
        return pltpu.make_async_remote_copy(
            src_ref=slot(r, p), dst_ref=slot(r, p),
            send_sem=down_send.at[r, p], recv_sem=kv_recv.at[r, p],
            device_id=plane_id(plane - 1), device_id_type=MESH)

    def out_copy(r):
        return pltpu.make_async_remote_copy(
            src_ref=o_buf.at[r], dst_ref=out_ref.at[:, lanes(me, wide)],
            send_sem=o_send.at[r], recv_sem=o_recv.at[me],
            device_id=member_id(r), device_id_type=MESH)

    def arrived(ref, sem):
        pltpu.make_async_copy(ref, ref, sem).wait()

    has_up = plane + 1 < planes
    has_down = plane > 0

    barrier = pltpu.get_barrier_semaphore()
    for j in range(1, members):
        pl.semaphore_signal(barrier, inc=1, device_id=member_id((me + j) % members),
                            device_id_type=MESH)

    @pl.when(has_up)
    def _():
        pl.semaphore_signal(barrier, inc=1, device_id=plane_id(plane + 1), device_id_type=MESH)

    @pl.when(has_down)
    def _():
        pl.semaphore_signal(barrier, inc=1, device_id=plane_id(plane - 1), device_id_type=MESH)

    pl.semaphore_wait(barrier, members - 1 + has_up.astype(jnp.int32) + has_down.astype(jnp.int32))

    for j in range(1, members):
        kv_copy(j).start()
    own_kv = pltpu.make_async_copy(
        kv_ref.at[:, lanes(me, pair)], slot(me, plane), kv_recv.at[me, plane])
    own_kv.start()
    for j in range(1, members):
        q_copy(j).start()
    own_q = pltpu.make_async_copy(q_ref.at[:, lanes(me, wide)], q_buf.at[me], q_recv.at[me])
    own_q.start()

    def gather(r, level):
        if level == 0:
            arrived(slot(r, plane), kv_recv.at[r, plane])

            @pl.when(has_up)
            def _():
                pass_up(r, plane).start()

            @pl.when(has_down)
            def _():
                pass_down(r, plane).start()
            return

        @pl.when(plane >= level)
        def _():
            p = plane - level
            arrived(slot(r, p), kv_recv.at[r, p])

            @pl.when(has_up)
            def _():
                pass_up(r, p).start()

        @pl.when(plane + level < planes)
        def _():
            p = plane + level
            arrived(slot(r, p), kv_recv.at[r, p])

            @pl.when(has_down)
            def _():
                pass_down(r, p).start()

    def gather_all(r):
        for level in range(planes):
            gather(r, level)

    factor = math.log2(math.e) / math.sqrt(dim)

    def absorb(r, c, masked):
        q = jnp.concatenate(
            [q_buf[r, :, g * dim:(g + 1) * dim] for g in range(group)], axis=0)
        kv = kv_buf[pl.ds(pl.multiple_of(c * keys, keys), keys), :]
        scores = lax.dot_general(q, kv[:, :dim], (((1,), (1,)), ((), ())),
                                 preferred_element_type=jnp.float32)
        if masked:
            t = lax.broadcasted_iota(jnp.int32, (block, keys), 0) + plane * block
            s = lax.broadcasted_iota(jnp.int32, (block, keys), 1)
            allowed = jnp.concatenate([s - t] * group, axis=0) <= 0
            scores = jnp.where(allowed, scores, -1e30)
        old = m_ref[...]
        new = jnp.maximum(old, jnp.max(scores, axis=1, keepdims=True))
        m_ref[...] = new
        fade = jnp.exp2((old - new) * factor)
        weights = jnp.exp2((scores - new[:, :1]) * factor)
        high = weights.astype(jnp.bfloat16)
        low = (weights - high.astype(jnp.float32)).astype(jnp.bfloat16)
        values = jnp.concatenate([kv[:, dim:], jnp.ones((keys, dim), jnp.bfloat16)], axis=1)
        mixed = jnp.dot(high, values, preferred_element_type=jnp.float32)
        mixed += jnp.dot(low, values, preferred_element_type=jnp.float32)
        acc_ref[...] = acc_ref[...] * jnp.concatenate([fade, fade], axis=1) + mixed

    early = min(3, members)
    for r in range(early):
        gather_all(r)

    def one_block(r, carry):
        arrived(q_buf.at[r], q_recv.at[r])
        m_ref[...] = jnp.full_like(m_ref, -1e30)
        acc_ref[...] = jnp.zeros_like(acc_ref)

        @pl.when((r < 5) & (r % 2 == 1) & ((r + 5) // 2 < members))
        def _():
            gather_all((r + 5) // 2)

        def past(c, carry):
            absorb(r, c, False)
            for level in range(planes):
                @pl.when((r >= 5) & (c == level))
                def _(level=level):
                    gather(r, level)
            return carry

        lax.fori_loop(0, r, past, 0)
        for level in range(planes):
            @pl.when((r >= 5) & (level >= r))
            def _(level=level):
                gather(r, level)
        absorb(r, r, True)
        result = (acc_ref[:, :dim] / acc_ref[:, dim:]).astype(jnp.bfloat16)
        for g in range(group):
            o_buf[r, :, g * dim:(g + 1) * dim] = result[g * block:(g + 1) * block]

        @pl.when(r != me)
        def _():
            out_copy(r).start()

        @pl.when(r == me)
        def _():
            pltpu.make_async_copy(o_buf.at[r], out_ref.at[:, lanes(me, wide)],
                                  o_recv.at[me]).start()
        return carry

    lax.fori_loop(0, members, one_block, 0)

    for j in range(1, members):
        kv_copy(j).wait_send()
        q_copy(j).wait_send()

    def finish(r, carry):
        for p in range(planes):
            @pl.when(has_up & (p <= plane))
            def _(p=p):
                pass_up(r, p).wait_send()

            @pl.when(has_down & (p >= plane))
            def _(p=p):
                pass_down(r, p).wait_send()

        @pl.when(r != me)
        def _():
            out_copy(r).wait_send()

        arrived(out_ref.at[:, lanes(r, wide)], o_recv.at[r])
        return carry

    lax.fori_loop(0, members, finish, 0)


def shards(head_n, inner_n, outer_n, q, k, v):
    block, heads, dim = q.shape
    kv_heads = k.shape[1]
    split = kv_heads // head_n
    assert split * head_n == kv_heads and inner_n % split == 0
    members = kv_heads
    planes = (inner_n // split) * outer_n
    group = heads // kv_heads
    sizes = (head_n, inner_n, outer_n, split, members, planes, block, group, dim)
    rows = group * block
    tokens = members * planes * block
    wide = group * dim
    q2 = q.reshape(block, heads * dim)
    kv2 = jnp.stack([k, v], axis=2).reshape(block, kv_heads * 2 * dim)
    dma = pltpu.SemaphoreType.DMA
    pairs = tokens * rows * planes * members // (2 * members * planes) * members
    out = pl.pallas_call(
        functools.partial(kernel, sizes),
        out_shape=jax.ShapeDtypeStruct((block, heads * dim), jnp.bfloat16),
        in_specs=[pl.BlockSpec(memory_space=pltpu.VMEM)] * 2,
        out_specs=pl.BlockSpec(memory_space=pltpu.VMEM),
        scratch_shapes=[
            pltpu.VMEM((members, block, wide), jnp.bfloat16),
            pltpu.VMEM((tokens, 2 * dim), jnp.bfloat16),
            pltpu.VMEM((members, block, wide), jnp.bfloat16),
            pltpu.VMEM((rows, dim), jnp.float32),
            pltpu.VMEM((rows, 2 * dim), jnp.float32),
            dma((members,)), dma((members,)),
            dma((members,)), dma((members, planes)),
            dma((members, planes)), dma((members, planes)),
            dma((members,)), dma((members,)),
        ],
        compiler_params=pltpu.CompilerParams(
            collective_id=0, has_side_effects=True, vmem_limit_bytes=60 * 1024 * 1024),
        cost_estimate=pl.CostEstimate(
            flops=6 * pairs * dim, bytes_accessed=4 * tokens * dim, transcendentals=pairs),
    )(q2, kv2)
    return out.reshape(block, heads, dim)


def solution(mesh):
    placed = P(("head", "inner", "outer"), None, None)
    sizes = [mesh.shape[name] for name in ("head", "inner", "outer")]
    return jax.shard_map(
        functools.partial(shards, *sizes),
        mesh=mesh,
        in_specs=(placed, placed, placed),
        out_specs=placed,
        check_vma=False,
    )
```

time: 205 us -> 143 us (0.70); the launches traced: 201 us -> 142 us
  Pallas kernels: 0 us -> 135 us
  matrix products: 80.9 us -> 0 us
  waiting for transfers between devices: 49.6 us -> 0 us
  starting transfers between devices: 20.4 us -> 0 us
  blocking collectives: 19.3 us -> 0 us
  other arithmetic: 18.3 us -> 1.08 us
  local copies, waits for them, and re-layouts: 12.1 us -> 5.86 us
    pallas_call x0 -> x1, Pallas kernels: none -> 135 us  [shards(): pl.pallas_call(functools.partial(kernel, sizes), out_shape=jax.ShapeDtype...]
    dot_general x16 -> x0, matrix products: 80.9 us -> none  [the longest x8 68.5 us: absorb(): jnp.einsum('kgts,skd->kgtd', weights, value_block.astype(jnp.float32), pr...]
    ppermute x7 -> x0, waiting for transfers between devices: 33.1 us -> none  [passed_along(): return lax.ppermute(x, axis, [(i, (i + by) % size) for i in range(size)])]
    all_to_all x1 -> x0, blocking collectives: 19.3 us -> none  [shards(): lax.all_to_all(result, 'head', split_axis=0, concat_axis=1, tiled=True)]
    all_to_all x3 -> x0, waiting for transfers between devices: 16.5 us -> none  [the longest x1 12.4 us: shards(): lax.all_to_all(rotated_asking_matrix, 'head', split_axis=1, concat_axis=0...]
    reduce_sum x4 -> x0, other arithmetic: 16.4 us -> none  [absorb(): run_sum = run_sum * factor + jnp.sum(weights, axis=-1)]
    all_to_all x3 -> x0, starting transfers between devices: 14.7 us -> none  [the longest x1 5.33 us: shards(): lax.all_to_all(rotated_asking_matrix, 'head', split_axis=1, concat_axis=0...]
    ppermute x7 -> x0, starting transfers between devices: 5.6 us -> none  [passed_along(): return lax.ppermute(x, axis, [(i, (i + by) % size) for i in range(size)])]
  transfers between devices with their start and end apart: 10 -> 0, of which waited for: 7 -> 0; matrix products, arithmetic and copies ran while one was open for 40% -> 0% of each run, Pallas kernels for 0% -> 0%
where the time goes in v1:
time: 143 us; the launch traced here: 142 us
  Pallas kernels  135 us (94%)
  local copies, waits for them, and re-layouts  5.86 us (4%)
    pallas_call x1, Pallas kernels, shards(): pl.pallas_call(functools.partial(kernel, sizes), out_shape=jax.ShapeDtype...  135 us
    unnamed x4, local copies, waits for them, and re-layouts  3.84 us

profile of v1, /device:TPU:7, one launch (start us, length us, event | category | flops | bytes accessed | tf_op | source)
XLA Modules:
  0.0 142.3 jit_solution(10688806015635309896)
XLA Ops:
  0.0 1.1 pad_maximum_fusion
  1.1 0.0 copy-start
  1.1 0.8 copy.4
  1.9 1.2 reshape.10.kv_ref
  3.1 0.0 copy-done
  3.1 1.4 copy.8
  4.5 135.3 %shard_map.37 = bf16[128,4096]{1,0:T(8,128)(2,1)} custom-call(bf16[128,4096]{1,0:T(8,128)(2,1)} %bitcast.10, bf16[128,2048]{1,0:T(8,128)(2,1)} %reshape.10.kv_ref), custom_call_target="tpu_custom_call" | custom-call | flops 6442450944 | bytes 2097152 | tf_op jit(solution)/shard_map/pallas_call | solution.py:246
  139.9 2.4 %copy.6 = bf16[16,8,32,128]{3,2,1,0:T(8,128)(2,1)} copy(bf16[16,8,32,128]{3,1,2,0:T(8,128)(2,1)} %bitcast.9) | data formatting | bytes 2097152
Async XLA Ops:
  1.1 2.0 %copy-start = (bf16[128,32,128]{2,1,0:T(8,128)(2,1)S(1)}, bf16[128,32,128]{2,1,0:T(8,128)(2,1)}, u32[]{:S(2)}) copy-start(bf16[128,32,128]{2,1,0:T(8,128)(2,1)} %param.3) | copy-start | bytes 3145732

commit v2 on v1

--- a/solution.py
+++ b/solution.py
@@ -131,65 +131,67 @@
             def _():
                 pass_down(r, p).start()
 
-    def gather_all(r):
-        for level in range(planes):
-            gather(r, level)
+    def advance(t, part):
+        r = t + 1 if part == 0 else t - part
+
+        @pl.when((r >= 0) & (r < members))
+        def _():
+            gather(r, part)
 
     factor = math.log2(math.e) / math.sqrt(dim)
 
     def absorb(r, c, masked):
-        q = jnp.concatenate(
-            [q_buf[r, :, g * dim:(g + 1) * dim] for g in range(group)], axis=0)
         kv = kv_buf[pl.ds(pl.multiple_of(c * keys, keys), keys), :]
-        scores = lax.dot_general(q, kv[:, :dim], (((1,), (1,)), ((), ())),
+        values = jnp.concatenate(
+            [kv[:, dim:].T, jnp.ones((16, keys), jnp.bfloat16)], axis=0)
+        if masked:
+            t = lax.broadcasted_iota(jnp.int32, (keys, block), 1) + plane * block
+            s = lax.broadcasted_iota(jnp.int32, (keys, block), 0)
+            allowed = s <= t
+        q = jnp.concatenate([q_buf[r, :, g * dim:(g + 1) * dim] for g in range(group)], axis=0)
+        scores = lax.dot_general(kv[:, :dim], q, (((1,), (1,)), ((), ())),
                                  preferred_element_type=jnp.float32)
         if masked:
-            t = lax.broadcasted_iota(jnp.int32, (block, keys), 0) + plane * block
-            s = lax.broadcasted_iota(jnp.int32, (block, keys), 1)
-            allowed = jnp.concatenate([s - t] * group, axis=0) <= 0
-            scores = jnp.where(allowed, scores, -1e30)
-        old = m_ref[...]
-        new = jnp.maximum(old, jnp.max(scores, axis=1, keepdims=True))
-        m_ref[...] = new
+            scores = jnp.where(jnp.concatenate([allowed] * group, axis=1), scores, -1e30)
+        old = m_ref[:1, :]
+        new = jnp.maximum(old, jnp.max(scores, axis=0, keepdims=True))
+        m_ref[:1, :] = new
         fade = jnp.exp2((old - new) * factor)
-        weights = jnp.exp2((scores - new[:, :1]) * factor)
+        weights = jnp.exp2((scores - new) * factor)
         high = weights.astype(jnp.bfloat16)
         low = (weights - high.astype(jnp.float32)).astype(jnp.bfloat16)
-        values = jnp.concatenate([kv[:, dim:], jnp.ones((keys, dim), jnp.bfloat16)], axis=1)
-        mixed = jnp.dot(high, values, preferred_element_type=jnp.float32)
-        mixed += jnp.dot(low, values, preferred_element_type=jnp.float32)
-        acc_ref[...] = acc_ref[...] * jnp.concatenate([fade, fade], axis=1) + mixed
-
-    early = min(3, members)
-    for r in range(early):
-        gather_all(r)
+        mixed = jnp.dot(values, high, preferred_element_type=jnp.float32)
+        mixed += jnp.dot(values, low, preferred_element_type=jnp.float32)
+        acc_ref[...] = acc_ref[...] * fade + mixed
+
+    gather(0, 0)
+    for t in range(planes - 1):
+        for part in range(t + 1):
+            advance(jnp.int32(t), part)
 
     def one_block(r, carry):
         arrived(q_buf.at[r], q_recv.at[r])
         m_ref[...] = jnp.full_like(m_ref, -1e30)
         acc_ref[...] = jnp.zeros_like(acc_ref)
 
-        @pl.when((r < 5) & (r % 2 == 1) & ((r + 5) // 2 < members))
-        def _():
-            gather_all((r + 5) // 2)
-
         def past(c, carry):
             absorb(r, c, False)
             for level in range(planes):
-                @pl.when((r >= 5) & (c == level))
+                @pl.when(c == level)
                 def _(level=level):
-                    gather(r, level)
+                    advance(r + planes - 1, level)
             return carry
 
         lax.fori_loop(0, r, past, 0)
         for level in range(planes):
-            @pl.when((r >= 5) & (level >= r))
+            @pl.when(level >= r)
             def _(level=level):
-                gather(r, level)
+                advance(r + planes - 1, level)
         absorb(r, r, True)
-        result = (acc_ref[:, :dim] / acc_ref[:, dim:]).astype(jnp.bfloat16)
         for g in range(group):
-            o_buf[r, :, g * dim:(g + 1) * dim] = result[g * block:(g + 1) * block]
+            at = pl.ds(g * block, block)
+            result = acc_ref[:dim, at] / acc_ref[dim:dim + 1, at]
+            o_buf[r, :, g * dim:(g + 1) * dim] = result.T.astype(jnp.bfloat16)
 
         @pl.when(r != me)
         def _():
@@ -252,8 +254,8 @@
             pltpu.VMEM((members, block, wide), jnp.bfloat16),
             pltpu.VMEM((tokens, 2 * dim), jnp.bfloat16),
             pltpu.VMEM((members, block, wide), jnp.bfloat16),
-            pltpu.VMEM((rows, dim), jnp.float32),
-            pltpu.VMEM((rows, 2 * dim), jnp.float32),
+            pltpu.VMEM((8, rows), jnp.float32),
+            pltpu.VMEM((dim + 16, rows), jnp.float32),
             dma((members,)), dma((members,)),
             dma((members,)), dma((members, planes)),
             dma((members, planes)), dma((members, planes)),

time: 143 us -> 74.3 us (0.52)
  Pallas kernels: 135 us -> 66.6 us
    pallas_call x1, Pallas kernels: 135 us -> 66.6 us  [shards(): pl.pallas_call(functools.partial(kernel, sizes), out_shape=jax.ShapeDtype...]
where the time goes in v2:
time: 74.3 us; the launch traced here: 73.6 us
  Pallas kernels  66.6 us (90%)
  local copies, waits for them, and re-layouts  5.86 us (8%)
  other arithmetic  1.08 us (1%)
    pallas_call x1, Pallas kernels, shards(): pl.pallas_call(functools.partial(kernel, sizes), out_shape=jax.ShapeDtype...  66.6 us
    unnamed x4, local copies, waits for them, and re-layouts  3.84 us

profile of v2, /device:TPU:7, one launch (start us, length us, event | category | flops | bytes accessed | tf_op | source)
XLA Modules:
  0.0 73.6 jit_solution(3960126453894135514)
XLA Ops:
  0.0 1.1 %pad_maximum_fusion = bf16[128,8,2,128]{3,1,0,2:T(8,128)(2,1)S(1)} fusion(bf16[128,8,1,128]{3,1,0,2:T(8,128)(2,1)} %bitcast.11, bf16[128,8,1,128]{3,1,0,2:T(8,128)(2,1)} %bitcast.12), kind=kLoop, calls=%fused_computation.1 | loop fusion | flops 262144 | bytes 1048576 | tf_op jit(solution)/shard_map/stack | solution.py:245
  1.1 0.0 copy-start
  1.1 0.8 %copy.4 = bf16[128,8,2,128]{3,2,1,0:T(2,128)(2,1)S(1)} copy(bf16[128,8,2,128]{3,1,0,2:T(8,128)(2,1)S(1)} %pad_maximum_fusion) | data formatting | bytes 1048576 | tf_op jit(solution)/shard_map/stack | solution.py:245
  1.9 1.2 %reshape.10.kv_ref = bf16[128,2048]{1,0:T(8,128)(2,1)} reshape(bf16[128,8,2,128]{3,2,1,0:T(2,128)(2,1)S(1)} %copy.4) | data formatting | bytes 1048576 | tf_op jit(solution)/shard_map/reshape | solution.py:245
  3.1 0.0 copy-done
  3.1 1.4 %copy.8 = bf16[16,8,32,128]{3,1,2,0:T(8,128)(2,1)} copy(bf16[16,8,32,128]{3,2,1,0:T(8,128)(2,1)S(1)} %bitcast.8) | data formatting | bytes 2097152
  4.5 66.6 %shard_map.37 = bf16[128,4096]{1,0:T(8,128)(2,1)} custom-call(bf16[128,4096]{1,0:T(8,128)(2,1)} %bitcast.10, bf16[128,2048]{1,0:T(8,128)(2,1)} %reshape.10.kv_ref), custom_call_target="tpu_custom_call" | custom-call | flops 6442450944 | bytes 2097152 | tf_op jit(solution)/shard_map/pallas_call | solution.py:248
  71.2 2.4 %copy.6 = bf16[16,8,32,128]{3,2,1,0:T(8,128)(2,1)} copy(bf16[16,8,32,128]{3,1,2,0:T(8,128)(2,1)} %bitcast.9) | data formatting | bytes 2097152
Async XLA Ops:
  1.1 2.0 %copy-start = (bf16[128,32,128]{2,1,0:T(8,128)(2,1)S(1)}, bf16[128,32,128]{2,1,0:T(8,128)(2,1)}, u32[]{:S(2)}) copy-start(bf16[128,32,128]{2,1,0:T(8,128)(2,1)} %param.3) | copy-start | bytes 3145732

commit v3 on v2

--- a/solution.py
+++ b/solution.py
@@ -11,12 +11,11 @@
 MESH = pl.DeviceIdType.MESH
 
 
-def kernel(sizes, q_ref, kv_ref, out_ref, q_buf, kv_buf, o_buf, m_ref, acc_ref,
-           q_send, q_recv, kv_send, kv_recv, up_send, down_send, o_send, o_recv):
+def kernel(sizes, q_ref, k_ref, v_ref, out_ref, q_buf, kv_buf, o_buf, m_ref, acc_ref,
+           q_send, q_recv, k_send, v_send, k_recv, v_recv, kv_recv, up_send, down_send, o_send, o_recv):
     head_n, inner_n, outer_n, split, members, planes, block, group, dim = sizes
     rest = inner_n // split
     wide = group * dim
-    pair = 2 * dim
     rows = group * block
     keys = planes * block
     head = lax.axis_index("head")
@@ -35,13 +34,26 @@
         return pl.ds(pl.multiple_of(index * width, dim), width)
 
     def slot(r, p):
-        return kv_buf.at[pl.ds(pl.multiple_of((r * planes + p) * block, block), block), :]
-
-    def kv_copy(j):
+        return kv_buf.at[r * planes + p]
+
+    def k_half(r, p):
+        return kv_buf.at[r * planes + p, :, pl.ds(0, dim)]
+
+    def v_half(r, p):
+        return kv_buf.at[r * planes + p, :, pl.ds(dim, block)]
+
+    def k_copy(j):
         to = (me + j) % members
         return pltpu.make_async_remote_copy(
-            src_ref=kv_ref.at[:, lanes(to, pair)], dst_ref=slot(me, plane),
-            send_sem=kv_send.at[j], recv_sem=kv_recv.at[me, plane],
+            src_ref=k_ref.at[:, lanes(to, dim)], dst_ref=k_half(me, plane),
+            send_sem=k_send.at[j], recv_sem=k_recv.at[me],
+            device_id=member_id(to), device_id_type=MESH)
+
+    def v_copy(j):
+        to = (me + j) % members
+        return pltpu.make_async_remote_copy(
+            src_ref=v_ref.at[:, lanes(to, block)], dst_ref=v_half(me, plane),
+            send_sem=v_send.at[j], recv_sem=v_recv.at[me],
             device_id=member_id(to), device_id_type=MESH)
 
     def q_copy(j):
@@ -74,6 +86,11 @@
 
     has_up = plane + 1 < planes
     has_down = plane > 0
+
+    for p in range(1, planes):
+        @pl.when(p > plane)
+        def _(p=p):
+            kv_buf[(members - 1) * planes + p] = jnp.zeros((block, dim + block), jnp.bfloat16)
 
     barrier = pltpu.get_barrier_semaphore()
     for j in range(1, members):
@@ -91,10 +108,12 @@
     pl.semaphore_wait(barrier, members - 1 + has_up.astype(jnp.int32) + has_down.astype(jnp.int32))
 
     for j in range(1, members):
-        kv_copy(j).start()
-    own_kv = pltpu.make_async_copy(
-        kv_ref.at[:, lanes(me, pair)], slot(me, plane), kv_recv.at[me, plane])
-    own_kv.start()
+        k_copy(j).start()
+        v_copy(j).start()
+    own_k = pltpu.make_async_copy(k_ref.at[:, lanes(me, dim)], k_half(me, plane), k_recv.at[me])
+    own_k.start()
+    own_v = pltpu.make_async_copy(v_ref.at[:, lanes(me, block)], v_half(me, plane), v_recv.at[me])
+    own_v.start()
     for j in range(1, members):
         q_copy(j).start()
     own_q = pltpu.make_async_copy(q_ref.at[:, lanes(me, wide)], q_buf.at[me], q_recv.at[me])
@@ -102,13 +121,14 @@
 
     def gather(r, level):
         if level == 0:
-            arrived(slot(r, plane), kv_recv.at[r, plane])
+            arrived(k_half(r, plane), k_recv.at[r])
+            arrived(v_half(r, plane), v_recv.at[r])
 
             @pl.when(has_up)
             def _():
                 pass_up(r, plane).start()
 
-            @pl.when(has_down)
+            @pl.when(has_down & (r < members - 1))
             def _():
                 pass_down(r, plane).start()
             return
@@ -122,7 +142,7 @@
             def _():
                 pass_up(r, p).start()
 
-        @pl.when(plane + level < planes)
+        @pl.when((plane + level < planes) & (r < members - 1))
         def _():
             p = plane + level
             arrived(slot(r, p), kv_recv.at[r, p])
@@ -141,56 +161,74 @@
     factor = math.log2(math.e) / math.sqrt(dim)
 
     def absorb(r, c, masked):
-        kv = kv_buf[pl.ds(pl.multiple_of(c * keys, keys), keys), :]
-        values = jnp.concatenate(
-            [kv[:, dim:].T, jnp.ones((16, keys), jnp.bfloat16)], axis=0)
+        parts = [kv_buf[c * planes + p] for p in range(planes)]
+        looked = jnp.concatenate([part[:, :dim] for part in parts], axis=0)
+        values = jnp.concatenate([part[:, dim:] for part in parts], axis=1)
+        values = jnp.concatenate([values, jnp.ones((16, keys), jnp.bfloat16)], axis=0)
         if masked:
             t = lax.broadcasted_iota(jnp.int32, (keys, block), 1) + plane * block
             s = lax.broadcasted_iota(jnp.int32, (keys, block), 0)
             allowed = s <= t
         q = jnp.concatenate([q_buf[r, :, g * dim:(g + 1) * dim] for g in range(group)], axis=0)
-        scores = lax.dot_general(kv[:, :dim], q, (((1,), (1,)), ((), ())),
+        scores = lax.dot_general(looked, q, (((1,), (1,)), ((), ())),
                                  preferred_element_type=jnp.float32)
         if masked:
             scores = jnp.where(jnp.concatenate([allowed] * group, axis=1), scores, -1e30)
-        old = m_ref[:1, :]
+        old = m_ref[r, :1, :]
         new = jnp.maximum(old, jnp.max(scores, axis=0, keepdims=True))
-        m_ref[:1, :] = new
+        m_ref[r, :1, :] = new
         fade = jnp.exp2((old - new) * factor)
         weights = jnp.exp2((scores - new) * factor)
         high = weights.astype(jnp.bfloat16)
         low = (weights - high.astype(jnp.float32)).astype(jnp.bfloat16)
         mixed = jnp.dot(values, high, preferred_element_type=jnp.float32)
         mixed += jnp.dot(values, low, preferred_element_type=jnp.float32)
-        acc_ref[...] = acc_ref[...] * fade + mixed
-
+        acc_ref[r] = acc_ref[r] * fade + mixed
+
+    m_ref[...] = jnp.full_like(m_ref, -1e30)
+    acc_ref[...] = jnp.zeros_like(acc_ref)
     gather(0, 0)
     for t in range(planes - 1):
         for part in range(t + 1):
             advance(jnp.int32(t), part)
 
+    half = members // 2
+
     def one_block(r, carry):
-        arrived(q_buf.at[r], q_recv.at[r])
-        m_ref[...] = jnp.full_like(m_ref, -1e30)
-        acc_ref[...] = jnp.zeros_like(acc_ref)
-
-        def past(c, carry):
-            absorb(r, c, False)
+        @pl.when(r <= half)
+        def _():
+            arrived(q_buf.at[r], q_recv.at[r])
+
+        ahead = jnp.where(r >= 1, jnp.maximum(members - half - r, 0), 0)
+        first = jnp.maximum(r - half, 0)
+        count = ahead + r - first
+
+        def past(i, carry):
+            late = i < ahead
+            block_id = jnp.where(late, r + half + i, r)
+            chunk = jnp.where(late, r - 1, first + i - ahead)
+
+            @pl.when(late & (r == 1))
+            def _():
+                arrived(q_buf.at[block_id], q_recv.at[block_id])
+
+            absorb(block_id, chunk, False)
             for level in range(planes):
-                @pl.when(c == level)
+                @pl.when(i == level)
                 def _(level=level):
                     advance(r + planes - 1, level)
+
             return carry
 
-        lax.fori_loop(0, r, past, 0)
+        lax.fori_loop(0, count, past, 0)
         for level in range(planes):
-            @pl.when(level >= r)
+            @pl.when(level >= count)
             def _(level=level):
                 advance(r + planes - 1, level)
         absorb(r, r, True)
         for g in range(group):
             at = pl.ds(g * block, block)
-            result = acc_ref[:dim, at] / acc_ref[dim:dim + 1, at]
+            result = acc_ref[r, :dim, at] / acc_ref[r, dim:dim + 1, at]
             o_buf[r, :, g * dim:(g + 1) * dim] = result.T.astype(jnp.bfloat16)
 
         @pl.when(r != me)
@@ -206,7 +244,8 @@
     lax.fori_loop(0, members, one_block, 0)
 
     for j in range(1, members):
-        kv_copy(j).wait_send()
+        k_copy(j).wait_send()
+        v_copy(j).wait_send()
         q_copy(j).wait_send()
 
     def finish(r, carry):
@@ -215,7 +254,7 @@
             def _(p=p):
                 pass_up(r, p).wait_send()
 
-            @pl.when(has_down & (p >= plane))
+            @pl.when(has_down & (p >= plane) & (r < members - 1))
             def _(p=p):
                 pass_down(r, p).wait_send()
 
@@ -242,30 +281,32 @@
     tokens = members * planes * block
     wide = group * dim
     q2 = q.reshape(block, heads * dim)
-    kv2 = jnp.stack([k, v], axis=2).reshape(block, kv_heads * 2 * dim)
+    k2 = k.reshape(block, kv_heads * dim)
+    v2 = v.transpose(2, 1, 0).reshape(dim, kv_heads * block)
+    assert dim == block
     dma = pltpu.SemaphoreType.DMA
     pairs = tokens * rows * planes * members // (2 * members * planes) * members
     out = pl.pallas_call(
         functools.partial(kernel, sizes),
         out_shape=jax.ShapeDtypeStruct((block, heads * dim), jnp.bfloat16),
-        in_specs=[pl.BlockSpec(memory_space=pltpu.VMEM)] * 2,
+        in_specs=[pl.BlockSpec(memory_space=pltpu.VMEM)] * 3,
         out_specs=pl.BlockSpec(memory_space=pltpu.VMEM),
         scratch_shapes=[
             pltpu.VMEM((members, block, wide), jnp.bfloat16),
-            pltpu.VMEM((tokens, 2 * dim), jnp.bfloat16),
+            pltpu.VMEM((members * planes, block, dim + block), jnp.bfloat16),
             pltpu.VMEM((members, block, wide), jnp.bfloat16),
-            pltpu.VMEM((8, rows), jnp.float32),
-            pltpu.VMEM((dim + 16, rows), jnp.float32),
+            pltpu.VMEM((members, 8, rows), jnp.float32),
+            pltpu.VMEM((members, dim + 16, rows), jnp.float32),
             dma((members,)), dma((members,)),
-            dma((members,)), dma((members, planes)),
-            dma((members, planes)), dma((members, planes)),
+            dma((members,)), dma((members,)), dma((members,)), dma((members,)),
+            dma((members, planes)), dma((members, planes)), dma((members, planes)),
             dma((members,)), dma((members,)),
         ],
         compiler_params=pltpu.CompilerParams(
             collective_id=0, has_side_effects=True, vmem_limit_bytes=60 * 1024 * 1024),
         cost_estimate=pl.CostEstimate(
             flops=6 * pairs * dim, bytes_accessed=4 * tokens * dim, transcendentals=pairs),
-    )(q2, kv2)
+    )(q2, k2, v2)
     return out.reshape(block, heads, dim)
 
 

time: 74.3 us -> 69.8 us (0.939)
  Pallas kernels: 66.6 us -> 62.5 us
  local copies, waits for them, and re-layouts: 5.86 us -> 6.98 us
  other arithmetic: 1.08 us -> 0 us
    pallas_call x1, Pallas kernels: 66.6 us -> 62.5 us  [shards(): pl.pallas_call(functools.partial(kernel, sizes), out_shape=jax.ShapeDtype...]
    transpose x0 -> x1, local copies, waits for them, and re-layouts: none -> 1.29 us  [shards(): v2 = v.transpose(2, 1, 0).reshape(dim, kv_heads * block)]
    another operation x1 -> x0, other arithmetic: 1.08 us -> none  [shards(): kv2 = jnp.stack([k, v], axis=2).reshape(block, kv_heads * 2 * dim)]
    another operation x1 -> x0, local copies, waits for them, and re-layouts: 0.81 us -> none  [shards(): kv2 = jnp.stack([k, v], axis=2).reshape(block, kv_heads * 2 * dim)]
where the time goes in v3:
time: 69.8 us; the launch traced here: 69.5 us
  Pallas kernels  62.5 us (90%)
  local copies, waits for them, and re-layouts  6.98 us (10%)
    pallas_call x1, Pallas kernels, shards(): pl.pallas_call(functools.partial(kernel, sizes), out_shape=jax.ShapeDtype...  62.5 us
    unnamed x4, local copies, waits for them, and re-layouts  3.84 us
    reshape x1, local copies, waits for them, and re-layouts, shards(): v2 = v.transpose(2, 1, 0).reshape(dim, kv_heads * block)  1.84 us

profile of v3, /device:TPU:7, one launch (start us, length us, event | category | flops | bytes accessed | tf_op | source)
XLA Modules:
  0.0 69.5 jit_solution(146966359005159226)
XLA Ops:
  0.0 0.0 copy-start
  0.0 1.3 %copy.4 = bf16[128,8,128]{2,1,0:T(8,128)(2,1)S(1)} copy(bf16[128,8,128]{0,1,2:T(8,128)(2,1)} %bitcast.17) | data formatting | bytes 524288 | tf_op jit(solution)/shard_map/transpose | solution.py:285
  1.3 1.8 %copy_bitcast_fusion.1 = (bf16[128,1024]{1,0:T(8,128)(2,1)}, bf16[128,1024]{1,0:T(8,128)(2,1)}) fusion(bf16[16,8,8,128]{3,2,1,0:T(8,128)(2,1)S(1)} %bitcast.16, bf16[16,8,8,128]{3,2,1,0:T(8,128)(2,1)} %bitcast.18), kind=kLoop, calls=%fused_computation.1 | loop fusion | bytes 1048576 | tf_op jit(solution)/shard_map/reshape | solution.py:285
  3.1 0.0 copy-done
  3.1 1.4 %copy.12 = bf16[16,8,32,128]{3,1,2,0:T(8,128)(2,1)} copy(bf16[16,8,32,128]{3,2,1,0:T(8,128)(2,1)S(1)} %bitcast.13) | data formatting | bytes 2097152
  4.6 62.5 %shard_map.37 = bf16[128,4096]{1,0:T(8,128)(2,1)} custom-call(bf16[128,4096]{1,0:T(8,128)(2,1)} %bitcast.15, bf16[128,1024]{1,0:T(8,128)(2,1)} %get-tuple-element.6.k_ref, bf16[128,1024]{1,0:T(8,128)(2,1)} %get-tuple-element.5.v_ref), custom_call_target="tpu_custom_call" | custom-call | flops 6442450944 | bytes 2097152 | tf_op jit(solution)/shard_map/pallas_call | solution.py:289
  67.1 2.4 %copy.8 = bf16[16,8,32,128]{3,2,1,0:T(8,128)(2,1)} copy(bf16[16,8,32,128]{3,1,2,0:T(8,128)(2,1)} %bitcast.14) | data formatting | bytes 2097152
Async XLA Ops:
  0.0 3.1 %copy-start = (bf16[128,32,128]{2,1,0:T(8,128)(2,1)S(1)}, bf16[128,32,128]{2,1,0:T(8,128)(2,1)}, u32[]{:S(2)}) copy-start(bf16[128,32,128]{2,1,0:T(8,128)(2,1)} %param.3) | copy-start | bytes 3145732

commit v4 on v3

--- a/solution.py
+++ b/solution.py
@@ -289,7 +289,7 @@
     out = pl.pallas_call(
         functools.partial(kernel, sizes),
         out_shape=jax.ShapeDtypeStruct((block, heads * dim), jnp.bfloat16),
-        in_specs=[pl.BlockSpec(memory_space=pltpu.VMEM)] * 3,
+        in_specs=[pl.BlockSpec(memory_space=pl.ANY)] * 3,
         out_specs=pl.BlockSpec(memory_space=pltpu.VMEM),
         scratch_shapes=[
             pltpu.VMEM((members, block, wide), jnp.bfloat16),
@@ -303,7 +303,7 @@
             dma((members,)), dma((members,)),
         ],
         compiler_params=pltpu.CompilerParams(
-            collective_id=0, has_side_effects=True, vmem_limit_bytes=60 * 1024 * 1024),
+            collective_id=0, has_side_effects=True, vmem_limit_bytes=2 ** 24 + 16 * tokens * dim),
         cost_estimate=pl.CostEstimate(
             flops=6 * pairs * dim, bytes_accessed=4 * tokens * dim, transcendentals=pairs),
     )(q2, k2, v2)

time: 69.8 us -> 64.5 us (0.924)
  local copies, waits for them, and re-layouts: 6.98 us -> 3.97 us
  Pallas kernels: 62.5 us -> 60.4 us
    unnamed x4, local copies, waits for them, and re-layouts: 3.84 us -> 1.65 us
    pallas_call x1, Pallas kernels: 62.5 us -> 60.4 us  [shards(): pl.pallas_call(functools.partial(kernel, sizes), out_shape=jax.ShapeDtype...]
    reshape x1, local copies, waits for them, and re-layouts: 1.84 us -> 1.02 us  [shards(): v2 = v.transpose(2, 1, 0).reshape(dim, kv_heads * block)]
where the time goes in v4:
time: 64.5 us; the launch traced here: 64.4 us
  Pallas kernels  60.4 us (94%)
  local copies, waits for them, and re-layouts  3.97 us (6%)
    pallas_call x1, Pallas kernels, shards(): pl.pallas_call(functools.partial(kernel, sizes), out_shape=jax.ShapeDtype...  60.4 us
    unnamed x4, local copies, waits for them, and re-layouts  1.65 us
    transpose x1, local copies, waits for them, and re-layouts, shards(): v2 = v.transpose(2, 1, 0).reshape(dim, kv_heads * block)  1.29 us

profile of v4, /device:TPU:7, one launch (start us, length us, event | category | flops | bytes accessed | tf_op | source)
XLA Modules:
  0.0 64.4 jit_solution(5848582522551191783)
XLA Ops:
  0.0 0.0 copy-start
  0.0 1.3 %copy.4 = bf16[128,8,128]{2,1,0:T(8,128)(2,1)S(1)} copy(bf16[128,8,128]{0,1,2:T(8,128)(2,1)} %bitcast.17) | data formatting | bytes 524288 | tf_op jit(solution)/shard_map/transpose | solution.py:285
  1.3 1.0 %copy_bitcast_fusion.1 = (bf16[128,1024]{1,0:T(8,128)(2,1)S(1)}, bf16[128,1024]{1,0:T(8,128)(2,1)S(1)}) fusion(bf16[16,8,8,128]{3,2,1,0:T(8,128)(2,1)S(1)} %bitcast.16, bf16[16,8,8,128]{3,2,1,0:T(8,128)(2,1)} %bitcast.18), kind=kLoop, calls=%fused_computation.1 | loop fusion | bytes 1048576 | tf_op jit(solution)/shard_map/reshape | solution.py:285
  2.3 0.0 copy-done
  2.3 0.5 copy.12
  2.8 60.4 %shard_map.37 = bf16[128,4096]{1,0:T(8,128)(2,1)S(1)} custom-call(bf16[128,4096]{1,0:T(8,128)(2,1)S(1)} %bitcast.14, bf16[128,1024]{1,0:T(8,128)(2,1)S(1)} %get-tuple-element.6.k_ref, bf16[128,1024]{1,0:T(8,128)(2,1)S(1)} %get-tuple-element.5.v_ref), custom_call_target="tpu_custom_call" | custom-call | flops 6442450944 | bytes 2097152 | tf_op jit(solution)/shard_map/pallas_call | solution.py:289
  63.2 1.2 %copy.8 = bf16[16,8,32,128]{3,2,1,0:T(8,128)(2,1)} copy(bf16[16,8,32,128]{3,1,2,0:T(8,128)(2,1)S(1)} %bitcast.13) | data formatting | bytes 2097152
Async XLA Ops:
  0.0 2.3 %copy-start = (bf16[128,32,128]{2,1,0:T(8,128)(2,1)S(1)}, bf16[128,32,128]{2,1,0:T(8,128)(2,1)}, u32[]{:S(2)}) copy-start(bf16[128,32,128]{2,1,0:T(8,128)(2,1)} %param.3) | copy-start | bytes 3145732

commit v5 on v4

--- a/solution.py
+++ b/solution.py
@@ -181,8 +181,9 @@
         weights = jnp.exp2((scores - new) * factor)
         high = weights.astype(jnp.bfloat16)
         low = (weights - high.astype(jnp.float32)).astype(jnp.bfloat16)
-        mixed = jnp.dot(values, high, preferred_element_type=jnp.float32)
-        mixed += jnp.dot(values, low, preferred_element_type=jnp.float32)
+        mixed = jnp.dot(jnp.concatenate([values, values], axis=1),
+                        jnp.concatenate([high, low], axis=0),
+                        preferred_element_type=jnp.float32)
         acc_ref[r] = acc_ref[r] * fade + mixed
 
     m_ref[...] = jnp.full_like(m_ref, -1e30)

time: 64.5 us -> 62.7 us (0.972)
  Pallas kernels: 60.4 us -> 58.6 us
    pallas_call x1, Pallas kernels: 60.4 us -> 58.6 us  [shards(): pl.pallas_call(functools.partial(kernel, sizes), out_shape=jax.ShapeDtype...]
where the time goes in v5:
time: 62.7 us; the launch traced here: 62.6 us
  Pallas kernels  58.6 us (93%)
  local copies, waits for them, and re-layouts  3.97 us (6%)
    pallas_call x1, Pallas kernels, shards(): pl.pallas_call(functools.partial(kernel, sizes), out_shape=jax.ShapeDtype...  58.6 us
    unnamed x4, local copies, waits for them, and re-layouts  1.65 us
    transpose x1, local copies, waits for them, and re-layouts, shards(): v2 = v.transpose(2, 1, 0).reshape(dim, kv_heads * block)  1.29 us

profile of v5, /device:TPU:7, one launch (start us, length us, event | category | flops | bytes accessed | tf_op | source)
XLA Modules:
  0.0 62.6 jit_solution(6840942032761241375)
XLA Ops:
  0.0 0.0 copy-start
  0.0 1.3 %copy.4 = bf16[128,8,128]{2,1,0:T(8,128)(2,1)S(1)} copy(bf16[128,8,128]{0,1,2:T(8,128)(2,1)} %bitcast.17) | data formatting | bytes 524288 | tf_op jit(solution)/shard_map/transpose | solution.py:286
  1.3 1.0 %copy_bitcast_fusion.1 = (bf16[128,1024]{1,0:T(8,128)(2,1)S(1)}, bf16[128,1024]{1,0:T(8,128)(2,1)S(1)}) fusion(bf16[16,8,8,128]{3,2,1,0:T(8,128)(2,1)S(1)} %bitcast.16, bf16[16,8,8,128]{3,2,1,0:T(8,128)(2,1)} %bitcast.18), kind=kLoop, calls=%fused_computation.1 | loop fusion | bytes 1048576 | tf_op jit(solution)/shard_map/reshape | solution.py:286
  2.3 0.0 copy-done
  2.3 0.5 copy.12
  2.8 58.6 %shard_map.37 = bf16[128,4096]{1,0:T(8,128)(2,1)S(1)} custom-call(bf16[128,4096]{1,0:T(8,128)(2,1)S(1)} %bitcast.14, bf16[128,1024]{1,0:T(8,128)(2,1)S(1)} %get-tuple-element.6.k_ref, bf16[128,1024]{1,0:T(8,128)(2,1)S(1)} %get-tuple-element.5.v_ref), custom_call_target="tpu_custom_call" | custom-call | flops 6442450944 | bytes 2097152 | tf_op jit(solution)/shard_map/pallas_call | solution.py:290
  61.4 1.2 %copy.8 = bf16[16,8,32,128]{3,2,1,0:T(8,128)(2,1)} copy(bf16[16,8,32,128]{3,1,2,0:T(8,128)(2,1)S(1)} %bitcast.13) | data formatting | bytes 2097152
Async XLA Ops:
  0.0 2.3 %copy-start = (bf16[128,32,128]{2,1,0:T(8,128)(2,1)S(1)}, bf16[128,32,128]{2,1,0:T(8,128)(2,1)}, u32[]{:S(2)}) copy-start(bf16[128,32,128]{2,1,0:T(8,128)(2,1)} %param.3) | copy-start | bytes 3145732
